TPU v7x, 32 devices: a whole 2x2x4 slice. The times are simulated.
32 devices in a mesh: section: 4 (over y, x), dp: 8 (over z, core).
Axes of the slice: x: 2, y: 2, z: 4, core: 2. Of those that a mesh axis runs over, the one named last changes fastest.
Arguments:
- clip_pool: bfloat16 [256, 256, 512], P('dp'), may hold values from -8 to 8
- clip_index: int32 [8, 32], P(None, 'dp'), may hold values from 0 to 31, as said below
- batch_order: int32 [8], replicated, may hold values from 0 to 7, each once
- tap_weights: bfloat16 [4, 3, 512, 512], P('section'), may hold values from -0.15625 to 0.15625
- out_weights: bfloat16 [4, 512, 512], P('section'), may hold values from -0.25 to 0.25
- norm_gains: bfloat16 [4, 512], P('section'), may hold values from 0.099609375 to 1.8984375
- quant_weight: bfloat16 [512, 18], replicated, may hold values from -0.25 to 0.25
- quant_bias: float32 [18], replicated, may hold values from -3 to 3
- post_weight: bfloat16 [18, 512], replicated, may hold values from -1.5 to 1.5
Outputs:
- row_error: float32 [8, 32, 256], P('section', 'dp')
- entropy_loss: float32 [8], replicated
Inputs may be any that keep to these rules, and one draw needn't show every extreme that they name: `clip_index`: entries index the clips of the replica that holds the column; over all 8 micro-batches, the 4 columns of one replica name each of its 32 clips exactly once. `batch_order`: each micro-batch number 0 to 7 once.
All inputs are finite; a program needn't handle non-finite values.
Results may differ from a plain program's by a relative error of at most 0.0015.
Values may be sent and summed in bfloat16 or wider, within the bound.
A program may use at most 128 MiB of HBM per device.

v0:
```python
import jax
import jax.numpy as jnp
from jax import lax
from jax.sharding import PartitionSpec as P

SPATIAL = 64
norm_eps = 1e-06
quant_section = 1


def run_block(current, tap_set, out_weight, gain_row):
    clip_count, row_count, channels = current.shape
    widened = current.astype(jnp.float32)
    scale = lax.rsqrt(jnp.mean(widened * widened, axis=-1, keepdims=True) + norm_eps)
    normed = (widened * scale * gain_row.astype(jnp.float32)).astype(jnp.bfloat16)
    flat = normed.reshape(-1, channels)
    mixed = jnp.zeros((clip_count, row_count, channels), jnp.float32)
    for k in range(tap_set.shape[0]):
        product = jnp.dot(flat, tap_set[k], preferred_element_type=jnp.float32).reshape(
            clip_count, row_count, channels
        )
        moved = jnp.pad(product, ((0, 0), (k * SPATIAL, 0), (0, 0)))[:, :row_count]
        mixed = mixed + moved
    activated = jax.nn.silu(mixed).astype(jnp.bfloat16)
    update = jnp.dot(
        activated.reshape(-1, channels), out_weight, preferred_element_type=jnp.float32
    )
    return (widened + update.reshape(clip_count, row_count, channels)).astype(jnp.bfloat16)


def quantize(current, quant_weight, quant_bias, post_weight):
    channels = current.shape[-1]
    logits = (
        jnp.dot(current.reshape(-1, channels), quant_weight, preferred_element_type=jnp.float32)
        + quant_bias
    )
    bit_prob = jax.nn.sigmoid(4.0 * logits)
    codes = (2.0 * bit_prob - 1.0).astype(jnp.bfloat16)
    quantized = jnp.dot(codes, post_weight, preferred_element_type=jnp.float32).astype(jnp.bfloat16)
    bit_sums = jnp.sum(bit_prob, axis=0)
    entropy_sum = -jnp.sum(
        bit_prob * jax.nn.log_sigmoid(4.0 * logits)
        + (1.0 - bit_prob) * jax.nn.log_sigmoid(-4.0 * logits)
    )
    return (quantized.reshape(current.shape), bit_sums, entropy_sum)


def squared_error(decoded, source):
    differ = decoded.astype(jnp.float32) - source.astype(jnp.float32)
    return jnp.mean(differ * differ, axis=-1)


def final_entropy(bit_buffer, entropy_buffer, batch_order, rows_total):
    marginal = bit_buffer / rows_total
    sample_entropy = entropy_buffer / rows_total
    averaged = jnp.zeros_like(marginal)
    running = marginal[batch_order[0]]
    for t in range(batch_order.shape[0]):
        if t > 0:
            running = 0.5 * running + 0.5 * marginal[batch_order[t]]
        averaged = averaged.at[batch_order[t]].set(running)
    smoothed = 0.05 + 0.9 * averaged
    code_entropy = -jnp.sum(
        smoothed * jnp.log(smoothed) + (1.0 - smoothed) * jnp.log(1.0 - smoothed), axis=-1
    )
    return sample_entropy - code_entropy


def on_device(
    clip_pool,
    clip_index,
    batch_order,
    tap_weights,
    out_weights,
    norm_gains,
    quant_weight,
    quant_bias,
    post_weight,
):
    section_id = lax.axis_index("section")
    sections = lax.axis_size("section")
    batches = batch_order.shape[0]
    clip_count = clip_index.shape[1]
    row_count = clip_pool.shape[1]
    rows_total = float(clip_count * lax.axis_size("dp") * row_count)
    bit_buffer = jnp.zeros((batches, quant_weight.shape[1]), jnp.float32)
    entropy_buffer = jnp.zeros((batches,), jnp.float32)
    all_taps, all_out, all_gains = (
        lax.all_gather(tap_weights, "section", axis=0, tiled=True),
        lax.all_gather(out_weights, "section", axis=0, tiled=True),
        lax.all_gather(norm_gains, "section", axis=0, tiled=True),
    )
    per_section = batches // sections
    error_list = []
    for i in range(per_section):
        batch_slot = section_id * per_section + i
        source = jnp.take(clip_pool, clip_index[batch_slot], axis=0)
        current = source
        for s in range(sections):
            current = run_block(current, all_taps[s], all_out[s], all_gains[s])
            if s == quant_section:
                current, bit_sums, entropy_sum = quantize(
                    current, quant_weight, quant_bias, post_weight
                )
                bit_buffer = bit_buffer.at[batch_slot].add(bit_sums)
                entropy_buffer = entropy_buffer.at[batch_slot].add(entropy_sum)
        error_list.append(squared_error(current, source))
    bit_buffer, entropy_buffer = lax.psum((bit_buffer, entropy_buffer), ("section", "dp"))
    error_out = jnp.stack(error_list)
    losses = final_entropy(bit_buffer, entropy_buffer, batch_order, rows_total)
    return (error_out, losses)


def solution(mesh):
    placed = (
        P("dp", None, None),
        P(None, "dp"),
        P(),
        P("section", None, None, None),
        P("section", None, None),
        P("section", None),
        P(),
        P(),
        P(),
    )
    return jax.shard_map(
        on_device,
        mesh=mesh,
        in_specs=placed,
        out_specs=(P("section", "dp", None), P()),
        check_vma=False,
    )
```

profile of v0, /device:TPU:0, one launch (start us, length us, event | category | flops | bytes accessed | tf_op | source)
XLA Modules:
  0.0 263.3 jit_solution(17527668626507960612)
XLA Ops:
  7.2 0.7 all-gather.4.cloned.1.call-update
  8.0 0.7 all-gather.6.cloned.1.call-update
  8.7 0.7 fusion.181
  20.1 4.9 %gather_fusion = bf16[4,256,512]{2,1,0:T(8,128)(2,1)S(1)} fusion(bf16[32,256,512]{2,1,0:T(8,128)(2,1)} %param.35, s32[1024]{0:T(1024)S(1)} %pad_clamp_fusion.1), kind=kCustom, calls=%fused_computation.clone | custom fusion | bytes 2097168 | tf_op jit(solution)/shard_map/jit(_take)/gather | solution.py:97
  25.0 4.4 %gather_fusion.1 = bf16[4,256,512]{2,1,0:T(8,128)(2,1)S(1)} fusion(bf16[32,256,512]{2,1,0:T(8,128)(2,1)} %param.35, s32[1024]{0:T(1024)S(1)} %pad_clamp_fusion), kind=kCustom, calls=%fused_computation.1.clone | custom fusion | bytes 2097168 | tf_op jit(solution)/shard_map/jit(_take)/gather | solution.py:97
  34.6 9.3 %all-gather = bf16[4,1,512]{2,1,0:T(2,128)(2,1)S(1)} all-gather(bf16[1,1,512]{2,1,0:T(2,128)(2,1)S(1)} %bitcast.176), channel_id=1, replica_groups=mesh['section'=4,'dp'=8] {'section'}, dimensions={0}, use_global_device_ids=true | all-gather | bytes 5120 | tf_op jit(solution)/shard_map/all_gather | solution.py:91
  44.0 0.8 and_reduce_fusion.4
  44.8 0.9 and_reduce_fusion
  46.5 36.1 %all-gather.4.cloned.1.call-done = bf16[4,3,512,512]{3,2,1,0:T(8,128)(2,1)} async-done(((bf16[1,3,512,512]{3,2,1,0:T(8,128)(2,1)}), bf16[4,3,512,512]{3,2,1,0:T(8,128)(2,1)}) %all-gather.4.cloned.1.call-update) | async-done | bytes 6291472 | tf_op jit(solution)/shard_map/all_gather | solution.py:89
  82.7 3.1 %fusion.60 = f32[4,256,512]{2,1,0:T(8,128)} fusion(f32[4,256]{1,0:T(4,128)S(1)} %add_rsqrt_fusion.3, f32[512]{0:T(512)S(1)} %bitcast.189, bf16[4,3,512,512]{3,2,1,0:T(8,128)(2,1)} %all-gather.4.cloned.1.call-done, bf16[4,256,512]{2,1,0:T(8,128)(2,1)S(1)} %gather_fusion.1, pred[4]{0:T(512)(128)(4,1)S(1)} %get-tuple-element.203), kind=kOutput, calls=%fused_computation.107 | convolution fusion | flops 539492352 | bytes 3676164 | tf_op jit(solution)/shard_map/dot_general | solution.py:19
  85.8 3.2 %fusion.58 = f32[4,256,512]{2,1,0:T(8,128)} fusion(f32[4,256]{1,0:T(4,128)S(1)} %add_rsqrt_fusion.3, f32[512]{0:T(512)S(1)} %bitcast.190, bf16[4,3,512,512]{3,2,1,0:T(8,128)(2,1)} %all-gather.4.cloned.1.call-done, bf16[4,256,512]{2,1,0:T(8,128)(2,1)S(1)} %gather_fusion.1, pred[4]{0:T(512)(128)(4,1)S(1)} %get-tuple-element.203), kind=kOutput, calls=%fused_computation.106 | convolution fusion | flops 539492352 | bytes 3676164 | tf_op jit(solution)/shard_map/dot_general | solution.py:19
  89.0 30.7 %all-gather.6.cloned.1.call-done = bf16[4,512,512]{2,1,0:T(8,128)(2,1)} async-done(((bf16[1,512,512]{2,1,0:T(8,128)(2,1)}), bf16[4,512,512]{2,1,0:T(8,128)(2,1)}) %all-gather.6.cloned.1.call-update) | async-done | bytes 2097168 | tf_op jit(solution)/shard_map/all_gather | solution.py:90
  119.7 4.6 %fusion.24 = (f32[4,256]{1,0:T(4,128)S(1)}, bf16[4,256,512]{2,1,0:T(8,128)(2,1)}) fusion(bf16[4,512,512]{2,1,0:T(8,128)(2,1)} %all-gather.6.cloned.1.call-done, f32[4,256,512]{2,1,0:T(8,128)} %fusion.58, f32[4,256,512]{2,1,0:T(8,128)} %fusion.60, f32[4,256]{1,0:T(4,128)S(1)} %add_rsqrt_fusion.3, f32[512]{0:T(512)S(1)} %bitcast.191, ...), kind=kOutput, calls=%fused_computation.62 | convolution fusion | flops 1083702272 | bytes 8399872 | tf_op jit(solution)/shard_map/dot_general | solution.py:25
  124.3 3.5 %fusion.54 = f32[4,256,512]{2,1,0:T(8,128)} fusion(bf16[4,256,512]{2,1,0:T(8,128)(2,1)} %get-tuple-element.188, f32[4,256]{1,0:T(4,128)S(1)} %add_rsqrt_fusion.2, f32[512]{0:T(512)S(1)} %bitcast.183, bf16[4,3,512,512]{3,2,1,0:T(8,128)(2,1)} %all-gather.4.cloned.1.call-done), kind=kOutput, calls=%fused_computation.105 | convolution fusion | flops 538968064 | bytes 3676160 | tf_op jit(solution)/shard_map/dot_general | solution.py:19
  127.9 3.2 %fusion.52 = f32[4,256,512]{2,1,0:T(8,128)} fusion(bf16[4,256,512]{2,1,0:T(8,128)(2,1)S(1)} %copy-done.16, f32[4,256]{1,0:T(4,128)S(1)} %add_rsqrt_fusion.2, f32[512]{0:T(512)S(1)} %bitcast.184, bf16[4,3,512,512]{3,2,1,0:T(8,128)(2,1)} %all-gather.4.cloned.1.call-done), kind=kOutput, calls=%fused_computation.104 | convolution fusion | flops 538968064 | bytes 3676160 | tf_op jit(solution)/shard_map/dot_general | solution.py:19
  131.1 5.2 %fusion.27 = bf16[4,256,512]{2,1,0:T(8,128)(2,1)} fusion(bf16[4,256,512]{2,1,0:T(8,128)(2,1)} %get-tuple-element.188, f32[4,256,512]{2,1,0:T(8,128)} %fusion.52, f32[4,256,512]{2,1,0:T(8,128)} %fusion.54, f32[4,256]{1,0:T(4,128)S(1)} %add_rsqrt_fusion.2, f32[512]{0:T(512)S(1)} %bitcast.185, bf16[4,3,512,512]{3,2,1,0:T(8,128)(2,1)} %all-gather.4.cloned.1.call-done, ...), kind=kOutput, calls=%fused_computation.65 | convolution fusion | flops 1081081856 | bytes 8394752 | tf_op jit(solution)/shard_map/dot_general | solution.py:25
  136.2 2.4 fusion.131
  139.3 3.2 %fusion.104 = f32[4,256,512]{2,1,0:T(8,128)} fusion(f32[512]{0:T(512)S(1)} %bitcast.192, f32[4,256]{1,0:T(4,128)S(1)} %add_rsqrt_fusion.7, bf16[4,3,512,512]{3,2,1,0:T(8,128)(2,1)} %all-gather.4.cloned.1.call-done, bf16[4,256,512]{2,1,0:T(8,128)(2,1)S(1)} %gather_fusion, pred[4]{0:T(512)(128)(4,1)S(1)} %get-tuple-element.204), kind=kOutput, calls=%fused_computation.135 | convolution fusion | flops 539492352 | bytes 3676164 | tf_op jit(solution)/shard_map/dot_general | solution.py:19
  142.5 3.1 %fusion.106 = f32[4,256,512]{2,1,0:T(8,128)} fusion(f32[512]{0:T(512)S(1)} %bitcast.193, f32[4,256]{1,0:T(4,128)S(1)} %add_rsqrt_fusion.7, bf16[4,3,512,512]{3,2,1,0:T(8,128)(2,1)} %all-gather.4.cloned.1.call-done, bf16[4,256,512]{2,1,0:T(8,128)(2,1)S(1)} %gather_fusion, pred[4]{0:T(512)(128)(4,1)S(1)} %get-tuple-element.204), kind=kOutput, calls=%fused_computation.136 | convolution fusion | flops 539492352 | bytes 3676164 | tf_op jit(solution)/shard_map/dot_general | solution.py:19
  145.6 4.6 %fusion.16 = (f32[4,256]{1,0:T(4,128)S(1)}, bf16[4,256,512]{2,1,0:T(8,128)(2,1)}) fusion(bf16[4,512,512]{2,1,0:T(8,128)(2,1)} %all-gather.6.cloned.1.call-done, f32[4,256,512]{2,1,0:T(8,128)} %fusion.104, f32[4,256,512]{2,1,0:T(8,128)} %fusion.106, f32[512]{0:T(512)S(1)} %bitcast.194, f32[4,256]{1,0:T(4,128)S(1)} %add_rsqrt_fusion.7, ...), kind=kOutput, calls=%fused_computation.54 | convolution fusion | flops 1083702272 | bytes 8399872 | tf_op jit(solution)/shard_map/dot_general | solution.py:25
  150.2 3.6 %fusion.82 = f32[4,256,512]{2,1,0:T(8,128)} fusion(bf16[4,256,512]{2,1,0:T(8,128)(2,1)} %get-tuple-element.190, f32[512]{0:T(512)S(1)} %bitcast.186, f32[4,256]{1,0:T(4,128)S(1)} %add_rsqrt_fusion.6, bf16[4,3,512,512]{3,2,1,0:T(8,128)(2,1)} %all-gather.4.cloned.1.call-done), kind=kOutput, calls=%fused_computation.119 | convolution fusion | flops 538968064 | bytes 3676160 | tf_op jit(solution)/shard_map/dot_general | solution.py:19
  153.8 3.1 %fusion.84 = f32[4,256,512]{2,1,0:T(8,128)} fusion(bf16[4,256,512]{2,1,0:T(8,128)(2,1)S(1)} %copy-done.15, f32[512]{0:T(512)S(1)} %bitcast.187, f32[4,256]{1,0:T(4,128)S(1)} %add_rsqrt_fusion.6, bf16[4,3,512,512]{3,2,1,0:T(8,128)(2,1)} %all-gather.4.cloned.1.call-done), kind=kOutput, calls=%fused_computation.120 | convolution fusion | flops 538968064 | bytes 3676160 | tf_op jit(solution)/shard_map/dot_general | solution.py:19
  156.9 4.3 %fusion.19 = bf16[4,256,512]{2,1,0:T(8,128)(2,1)S(1)} fusion(bf16[4,256,512]{2,1,0:T(8,128)(2,1)} %get-tuple-element.190, f32[4,256,512]{2,1,0:T(8,128)} %fusion.82, f32[4,256,512]{2,1,0:T(8,128)} %fusion.84, f32[512]{0:T(512)S(1)} %bitcast.188, f32[4,256]{1,0:T(4,128)S(1)} %add_rsqrt_fusion.6, bf16[4,3,512,512]{3,2,1,0:T(8,128)(2,1)} %all-gather.4.cloned.1.call-done, ...), kind=kOutput, calls=%fused_computation.57 | convolution fusion | flops 1081081856 | bytes 8394752 | tf_op jit(solution)/shard_map/dot_general | solution.py:25
  161.3 1.1 fusion.125
  163.6 0.7 broadcast_select_fusion.9
  164.6 39.3 %all-reduce.16 = (f32[8,18]{1,0:T(8,128)S(1)}, f32[8]{0:T(128)S(1)}) all-reduce(f32[8,18]{1,0:T(8,128)S(1)} %scatter-add.19, f32[8]{0:T(128)S(1)} %fusion.155), channel_id=1, replica_groups=mesh['section'=4,'dp'=8] {'section','dp'}, use_global_device_ids=true, to_apply=%region_18.20 | all-reduce | flops 152 | bytes 1216 | tf_op jit(solution)/shard_map/psum | solution.py:108
  203.9 0.7 broadcast_select_fusion.11
  204.7 0.6 broadcast_select_fusion.8
  205.3 0.7 broadcast_select_fusion.7
  206.1 0.6 broadcast_select_fusion.6
  206.7 0.6 broadcast_select_fusion.5
  207.4 0.7 broadcast_select_fusion.4
  208.1 0.7 broadcast_select_fusion.3
  208.9 0.6 broadcast_select_fusion.2
  211.6 0.6 copy-done.4
  212.2 3.1 %fusion.120 = f32[4,256,512]{2,1,0:T(8,128)} fusion(bf16[4,256,512]{2,1,0:T(8,128)(2,1)S(1)} %bitcast.170, bf16[4,3,512,512]{3,2,1,0:T(8,128)(2,1)} %all-gather.4.cloned.1.call-done), kind=kOutput, calls=%fused_computation.160 | convolution fusion | flops 536870912 | bytes 3670016 | tf_op jit(solution)/shard_map/dot_general | solution.py:19
  215.3 3.1 %fusion.118 = f32[4,256,512]{2,1,0:T(8,128)} fusion(bf16[4,256,512]{2,1,0:T(8,128)(2,1)S(1)} %bitcast.171, bf16[4,3,512,512]{3,2,1,0:T(8,128)(2,1)} %all-gather.4.cloned.1.call-done), kind=kOutput, calls=%fused_computation.158 | convolution fusion | flops 536870912 | bytes 3670016 | tf_op jit(solution)/shard_map/dot_general | solution.py:19
  218.4 5.2 %fusion.28 = (f32[4,256]{1,0:T(4,128)S(1)}, bf16[4,256,512]{2,1,0:T(8,128)(2,1)}) fusion(f32[4,256,512]{2,1,0:T(8,128)} %bitcast.174, bf16[4,512,512]{2,1,0:T(8,128)(2,1)} %all-gather.6.cloned.1.call-done, f32[4,256,512]{2,1,0:T(8,128)} %fusion.120, f32[4,256,512]{2,1,0:T(8,128)} %fusion.118, bf16[4,256,512]{2,1,0:T(8,128)(2,1)S(1)} %bitcast.172, ...), kind=kOutput, calls=%fused_computation.66 | convolution fusion | flops 1080032256 | bytes 9441280 | tf_op jit(solution)/shard_map/dot_general | solution.py:25
  223.6 3.5 %fusion.48 = f32[4,256,512]{2,1,0:T(8,128)} fusion(bf16[4,256,512]{2,1,0:T(8,128)(2,1)} %get-tuple-element.196, f32[4,256]{1,0:T(4,128)S(1)} %add_rsqrt_fusion, f32[512]{0:T(512)S(1)} %bitcast.177, bf16[4,3,512,512]{3,2,1,0:T(8,128)(2,1)} %all-gather.4.cloned.1.call-done), kind=kOutput, calls=%fused_computation.103 | convolution fusion | flops 538968064 | bytes 3676160 | tf_op jit(solution)/shard_map/dot_general | solution.py:19
  227.1 3.2 %fusion.46 = f32[4,256,512]{2,1,0:T(8,128)} fusion(bf16[4,256,512]{2,1,0:T(8,128)(2,1)S(1)} %copy-done.14, f32[4,256]{1,0:T(4,128)S(1)} %add_rsqrt_fusion, f32[512]{0:T(512)S(1)} %bitcast.178, bf16[4,3,512,512]{3,2,1,0:T(8,128)(2,1)} %all-gather.4.cloned.1.call-done), kind=kOutput, calls=%fused_computation.102 | convolution fusion | flops 538968064 | bytes 3676160 | tf_op jit(solution)/shard_map/dot_general | solution.py:19
  230.3 3.8 %fusion.43 = f32[4,256]{1,0:T(4,128)S(1)} fusion(f32[4,256,512]{2,1,0:T(8,128)} %fusion.46, f32[4,256,512]{2,1,0:T(8,128)} %fusion.48, bf16[4,256,512]{2,1,0:T(8,128)(2,1)S(1)} %copy-done.14, f32[4,256]{1,0:T(4,128)S(1)} %add_rsqrt_fusion, f32[512]{0:T(512)S(1)} %bitcast.179, bf16[4,3,512,512]{3,2,1,0:T(8,128)(2,1)} %all-gather.4.cloned.1.call-done, ...), kind=kOutput, calls=%fused_computation.81 | convolution fusion | flops 1084226560 | bytes 8399360 | tf_op jit(solution)/shard_map/dot_general | solution.py:25
  234.0 3.0 %fusion.121 = f32[4,256,512]{2,1,0:T(8,128)} fusion(bf16[4,256,512]{2,1,0:T(8,128)(2,1)S(1)} %bitcast.167, bf16[4,3,512,512]{3,2,1,0:T(8,128)(2,1)} %all-gather.4.cloned.1.call-done), kind=kOutput, calls=%fused_computation.161 | convolution fusion | flops 536870912 | bytes 3670016 | tf_op jit(solution)/shard_map/dot_general | solution.py:19
  237.1 3.3 %fusion.119 = f32[4,256,512]{2,1,0:T(8,128)} fusion(bf16[4,256,512]{2,1,0:T(8,128)(2,1)S(1)} %bitcast.168, bf16[4,3,512,512]{3,2,1,0:T(8,128)(2,1)} %all-gather.4.cloned.1.call-done), kind=kOutput, calls=%fused_computation.159 | convolution fusion | flops 536870912 | bytes 3670016 | tf_op jit(solution)/shard_map/dot_general | solution.py:19
  240.3 4.4 %fusion.20 = (f32[4,256]{1,0:T(4,128)S(1)}, bf16[4,256,512]{2,1,0:T(8,128)(2,1)}) fusion(f32[4,256,512]{2,1,0:T(8,128)S(1)} %bitcast.173, bf16[4,512,512]{2,1,0:T(8,128)(2,1)} %all-gather.6.cloned.1.call-done, f32[4,256,512]{2,1,0:T(8,128)} %fusion.121, f32[4,256,512]{2,1,0:T(8,128)} %fusion.119, bf16[4,256,512]{2,1,0:T(8,128)(2,1)S(1)} %bitcast.169, ...), kind=kOutput, calls=%fused_computation.58 | convolution fusion | flops 1080032256 | bytes 9441280 | tf_op jit(solution)/shard_map/dot_general | solution.py:25
  244.7 3.6 %fusion.68 = f32[4,256,512]{2,1,0:T(8,128)} fusion(bf16[4,256,512]{2,1,0:T(8,128)(2,1)} %get-tuple-element.198, f32[512]{0:T(512)S(1)} %bitcast.180, f32[4,256]{1,0:T(4,128)S(1)} %add_rsqrt_fusion.4, bf16[4,3,512,512]{3,2,1,0:T(8,128)(2,1)} %all-gather.4.cloned.1.call-done), kind=kOutput, calls=%fused_computation.111 | convolution fusion | flops 538968064 | bytes 3676160 | tf_op jit(solution)/shard_map/dot_general | solution.py:19
  248.4 3.2 %fusion.70 = f32[4,256,512]{2,1,0:T(8,128)} fusion(bf16[4,256,512]{2,1,0:T(8,128)(2,1)S(1)} %copy-done.13, f32[512]{0:T(512)S(1)} %bitcast.181, f32[4,256]{1,0:T(4,128)S(1)} %add_rsqrt_fusion.4, bf16[4,3,512,512]{3,2,1,0:T(8,128)(2,1)} %all-gather.4.cloned.1.call-done), kind=kOutput, calls=%fused_computation.112 | convolution fusion | flops 538968064 | bytes 3676160 | tf_op jit(solution)/shard_map/dot_general | solution.py:19
  251.6 3.8 %fusion.37 = f32[4,256]{1,0:T(4,128)S(1)} fusion(f32[4,256,512]{2,1,0:T(8,128)} %fusion.68, f32[4,256,512]{2,1,0:T(8,128)} %fusion.70, bf16[4,256,512]{2,1,0:T(8,128)(2,1)S(1)} %copy-done.13, f32[512]{0:T(512)S(1)} %bitcast.182, f32[4,256]{1,0:T(4,128)S(1)} %add_rsqrt_fusion.4, bf16[4,3,512,512]{3,2,1,0:T(8,128)(2,1)} %all-gather.4.cloned.1.call-done, ...), kind=kOutput, calls=%fused_computation.75 | convolution fusion | flops 1084226560 | bytes 8399360 | tf_op jit(solution)/shard_map/dot_general | solution.py:25
  255.8 0.6 pad_maximum_fusion
  (75 shorter events, 5.1 us)
Async XLA Ops:
  7.2 202.5 %copy-start = (bf16[18,512]{1,0:T(8,128)(2,1)S(1)}, bf16[18,512]{1,0:T(8,128)(2,1)}, u32[]{:S(2)}) copy-start(bf16[18,512]{1,0:T(8,128)(2,1)} %param.43) | copy-start | bytes 55300
  7.2 1.5 copy-start.7
  7.2 12.6 %copy-start.8 = (s32[8,4]{0,1:T(4,128)S(1)}, s32[8,4]{0,1:T(4,128)}, u32[]{:S(2)}) copy-start(s32[8,4]{0,1:T(4,128)} %param.36) | copy-start | bytes 388
  7.2 75.5 %all-gather.4.cloned.1.call-start = ((), (), s32[]{:S(2)}) async-start(), calls=%async_computation | async-start | bytes 7864320 | tf_op jit(solution)/shard_map/all_gather | solution.py:89
  7.9 111.8 %all-gather.6.cloned.1.call-start = ((), (), s32[]{:S(2)}) async-start(), calls=%async_computation.1 | async-start | bytes 2621440 | tf_op jit(solution)/shard_map/all_gather | solution.py:90
  20.1 14.6 %copy-start.10 = (bf16[1,512]{1,0:T(2,128)(2,1)S(1)}, bf16[1,512]{1,0:T(2,128)(2,1)}, u32[]{:S(2)}) copy-start(bf16[1,512]{1,0:T(2,128)(2,1)} %param.40) | copy-start | bytes 3076
  20.1 23.9 %copy-start.9 = (s32[2]{0:T(128)S(1)}, s32[2]{0:T(128)}, u32[]{:S(2)}) copy-start(s32[2]{0:T(128)} %constant.321.clone.1) | copy-start | bytes 28
  25.0 120.6 %copy-start.5 = (bf16[4,256,512]{2,1,0:T(8,128)(2,1)}, bf16[4,256,512]{2,1,0:T(8,128)(2,1)S(1)}, u32[]{:S(2)}) copy-start(bf16[4,256,512]{2,1,0:T(8,128)(2,1)S(1)} %gather_fusion) | copy-start | bytes 3145732
  124.3 3.5 %copy-start.16 = (bf16[4,256,512]{2,1,0:T(8,128)(2,1)S(1)}, bf16[4,256,512]{2,1,0:T(8,128)(2,1)}, u32[]{:S(2)}) copy-start(bf16[4,256,512]{2,1,0:T(8,128)(2,1)} %get-tuple-element.188) | copy-start | bytes 3145732
  131.1 5.2 %copy-start.11 = (bf16[512,18]{0,1:T(8,128)(2,1)S(1)}, bf16[512,18]{0,1:T(8,128)(2,1)}, u32[]{:S(2)}) copy-start(bf16[512,18]{0,1:T(8,128)(2,1)} %param.41) | copy-start | bytes 55300
  131.1 5.2 %copy-start.12 = (f32[18]{0:T(128)S(1)}, f32[18]{0:T(128)}, u32[]{:S(2)}) copy-start(f32[18]{0:T(128)} %param.42) | copy-start | bytes 220
  150.2 3.6 %copy-start.15 = (bf16[4,256,512]{2,1,0:T(8,128)(2,1)S(1)}, bf16[4,256,512]{2,1,0:T(8,128)(2,1)}, u32[]{:S(2)}) copy-start(bf16[4,256,512]{2,1,0:T(8,128)(2,1)} %get-tuple-element.190) | copy-start | bytes 3145732
  210.2 1.4 copy-start.2
  210.8 1.4 copy-start.4
  223.6 3.5 %copy-start.14 = (bf16[4,256,512]{2,1,0:T(8,128)(2,1)S(1)}, bf16[4,256,512]{2,1,0:T(8,128)(2,1)}, u32[]{:S(2)}) copy-start(bf16[4,256,512]{2,1,0:T(8,128)(2,1)} %get-tuple-element.196) | copy-start | bytes 3145732
  237.1 3.3 %copy-start.3 = (f32[1024,512]{1,0:T(8,128)S(1)}, f32[1024,512]{1,0:T(8,128)}, u32[]{:S(2)}) copy-start(f32[1024,512]{1,0:T(8,128)} %copy-done.2) | copy-start | bytes 6291460
  244.7 3.6 %copy-start.13 = (bf16[4,256,512]{2,1,0:T(8,128)(2,1)S(1)}, bf16[4,256,512]{2,1,0:T(8,128)(2,1)}, u32[]{:S(2)}) copy-start(bf16[4,256,512]{2,1,0:T(8,128)(2,1)} %get-tuple-element.198) | copy-start | bytes 3145732
  248.4 3.2 %copy-start.6 = (bf16[4,256,512]{2,1,0:T(8,128)(2,1)S(1)}, bf16[4,256,512]{2,1,0:T(8,128)(2,1)}, u32[]{:S(2)}) copy-start(bf16[4,256,512]{2,1,0:T(8,128)(2,1)} %copy-done.5) | copy-start | bytes 3145732
  251.5 4.9 %copy-start.1 = (bf16[18,512]{1,0:T(8,128)(2,1)S(1)}, bf16[18,512]{1,0:T(8,128)(2,1)}, u32[]{:S(2)}) copy-start(bf16[18,512]{1,0:T(8,128)(2,1)} %param.43) | copy-start | bytes 55300
Sparse Core Ops, SparseCore 0:
  9.9 72.7 all-gather.3
  84.5 35.1 all-gather.5
where the time goes:
time: 265 us; the launch traced here: 263 us
  matrix products  92.5 us (35%)
  waiting for transfers between devices  68.2 us (26%)
  blocking collectives  48.6 us (18%)
  between operations  31.2 us (12%)
  local copies, waits for them, and re-layouts  11.6 us (4%)
  other arithmetic  11.1 us (4%)
    dot_general x16, matrix products, run_block(): jnp.dot(flat, tap_set[k], preferred_element_type=jnp.float32)  52 us
    psum x1, blocking collectives, on_device(): lax.psum((bit_buffer, entropy_buffer), ('section', 'dp'))  39.3 us
    all_gather x1, waiting for transfers between devices, on_device(): lax.all_gather(tap_weights, 'section', axis=0, tiled=True)  36.1 us
    dot_general x8, matrix products, run_block(): jnp.dot(activated.reshape(-1, channels), out_weight, preferred_element_ty...  35.9 us
    all_gather x1, waiting for transfers between devices, on_device(): lax.all_gather(out_weights, 'section', axis=0, tiled=True)  30.7 us
    all_gather x1, blocking collectives, on_device(): lax.all_gather(norm_gains, 'section', axis=0, tiled=True)  9.32 us
    gather x2, local copies, waits for them, and re-layouts, on_device(): source = jnp.take(clip_pool, clip_index[batch_slot], axis=0)  9.28 us
    another operation x12, other arithmetic  8.18 us
  transfers between devices with their start and end apart: 2, of which 2 were waited for; matrix products, arithmetic and copies ran while one was open for 7% of the time, Pallas kernels for 0%

commit v1 on v0

--- a/solution.py
+++ b/solution.py
@@ -87,7 +87,10 @@
     entropy_buffer = jnp.zeros((batches,), jnp.float32)
     all_taps, all_out, all_gains = (
         lax.all_gather(tap_weights, "section", axis=0, tiled=True),
-        lax.all_gather(out_weights, "section", axis=0, tiled=True),
+        jnp.concatenate(
+            lax.all_to_all(jnp.stack([out_weights] * lax.axis_size("section")), "section", 0, 0),
+            axis=0,
+        ),
         lax.all_gather(norm_gains, "section", axis=0, tiled=True),
     )
     per_section = batches // sections

time: 265 us -> 254 us (0.958)
  waiting for transfers between devices: 68.2 us -> 36.9 us
  blocking collectives: 48.6 us -> 60.8 us
  starting transfers between devices: 0.08 us -> 5.36 us
    all_gather x1 -> x0, waiting for transfers between devices: 30.7 us -> none  [on_device(): lax.all_gather(out_weights, 'section', axis=0, tiled=True)]
    all_gather x1, blocking collectives: 9.32 us -> 21.5 us  [on_device(): lax.all_gather(norm_gains, 'section', axis=0, tiled=True)]
    all_to_all x0 -> x1, starting transfers between devices: none -> 5.32 us  [on_device(): lax.all_to_all(jnp.stack([out_weights] * lax.axis_size('section')), 'sect...]
  transfers between devices with their start and end apart: 2 -> 2, of which waited for: 2 -> 1; matrix products, arithmetic and copies ran while one was open for 7% -> 8% of each run, Pallas kernels for 0% -> 0%
where the time goes in v1:
time: 254 us; the launch traced here: 252 us
  matrix products  94.9 us (37%)
  blocking collectives  60.8 us (24%)
  waiting for transfers between devices  36.9 us (15%)
  between operations  30.4 us (12%)
  local copies, waits for them, and re-layouts  13.2 us (5%)
  other arithmetic  10.9 us (4%)
  starting transfers between devices  5.36 us (2%)
    dot_general x16, matrix products, run_block(): jnp.dot(flat, tap_set[k], preferred_element_type=jnp.float32)  52.2 us
    psum x1, blocking collectives, on_device(): lax.psum((bit_buffer, entropy_buffer), ('section', 'dp'))  39.3 us
    dot_general x8, matrix products, run_block(): jnp.dot(activated.reshape(-1, channels), out_weight, preferred_element_ty...  36.8 us
    all_gather x1, waiting for transfers between devices, on_device(): lax.all_gather(tap_weights, 'section', axis=0, tiled=True)  36.3 us
    all_gather x1, blocking collectives, on_device(): lax.all_gather(norm_gains, 'section', axis=0, tiled=True)  21.5 us
    gather x2, local copies, waits for them, and re-layouts, on_device(): source = jnp.take(clip_pool, clip_index[batch_slot], axis=0)  8.37 us
    another operation x12, other arithmetic  8.04 us
    all_to_all x1, starting transfers between devices, on_device(): lax.all_to_all(jnp.stack([out_weights] * lax.axis_size('section')), 'sect...  5.32 us
  transfers between devices with their start and end apart: 2, of which 1 were waited for; matrix products, arithmetic and copies ran while one was open for 8% of the time, Pallas kernels for 0%

profile of v1, /device:TPU:0, one launch (start us, length us, event | category | flops | bytes accessed | tf_op | source)
XLA Modules:
  0.0 252.5 jit_solution(12421077134038402218)
XLA Ops:
  7.2 0.7 all-gather.3.cloned.1.call-update
  7.9 2.6 %stack.4 = bf16[4,1,512,512]{3,2,1,0:T(8,128)(2,1)} broadcast(bf16[512,512]{1,0:T(8,128)(2,1)} %bitcast.180), dimensions={2,3} | broadcast | bytes 2621440 | tf_op jit(solution)/shard_map/stack | solution.py:91
  10.5 5.3 %all-to-all-start = ((bf16[4,1,512,512]{3,2,1,0:T(8,128)(2,1)}), bf16[4,1,512,512]{3,2,1,0:T(8,128)(2,1)}, u32[]{:S(2)}, u32[]{:S(2)}) async-start(bf16[4,1,512,512]{3,2,1,0:T(8,128)(2,1)} %stack.4), calls=%async_computation | async-start | bytes 4194304 | tf_op jit(solution)/shard_map/all_to_all | solution.py:91
  15.8 0.7 fusion.181
  26.7 4.0 %gather_fusion = bf16[4,256,512]{2,1,0:T(8,128)(2,1)S(1)} fusion(bf16[32,256,512]{2,1,0:T(8,128)(2,1)} %param.35, s32[1024]{0:T(1024)S(1)} %pad_clamp_fusion.1), kind=kCustom, calls=%fused_computation.clone | custom fusion | bytes 2097168 | tf_op jit(solution)/shard_map/jit(_take)/gather | solution.py:100
  30.7 4.4 %gather_fusion.1 = bf16[4,256,512]{2,1,0:T(8,128)(2,1)S(1)} fusion(bf16[32,256,512]{2,1,0:T(8,128)(2,1)} %param.35, s32[1024]{0:T(1024)S(1)} %pad_clamp_fusion), kind=kCustom, calls=%fused_computation.1.clone | custom fusion | bytes 2097168 | tf_op jit(solution)/shard_map/jit(_take)/gather | solution.py:100
  40.1 21.5 %all-gather = bf16[4,1,512]{2,1,0:T(2,128)(2,1)S(1)} all-gather(bf16[1,1,512]{2,1,0:T(2,128)(2,1)S(1)} %bitcast.182), channel_id=1, replica_groups=mesh['section'=4,'dp'=8] {'section'}, dimensions={0}, use_global_device_ids=true | all-gather | bytes 5120 | tf_op jit(solution)/shard_map/all_gather | solution.py:94
  61.6 0.9 and_reduce_fusion
  62.9 0.8 and_reduce_fusion.4
  64.1 36.3 %all-gather.3.cloned.1.call-done = bf16[4,3,512,512]{3,2,1,0:T(8,128)(2,1)} async-done(((bf16[1,3,512,512]{3,2,1,0:T(8,128)(2,1)}), bf16[4,3,512,512]{3,2,1,0:T(8,128)(2,1)}) %all-gather.3.cloned.1.call-update) | async-done | bytes 6291472 | tf_op jit(solution)/shard_map/all_gather | solution.py:89
  100.4 3.1 %fusion.104 = f32[4,256,512]{2,1,0:T(8,128)} fusion(f32[512]{0:T(512)S(1)} %bitcast.195, f32[4,256]{1,0:T(4,128)S(1)} %add_rsqrt_fusion.7, bf16[4,3,512,512]{3,2,1,0:T(8,128)(2,1)} %all-gather.3.cloned.1.call-done, bf16[4,256,512]{2,1,0:T(8,128)(2,1)S(1)} %gather_fusion, pred[4]{0:T(512)(128)(4,1)S(1)} %get-tuple-element.204), kind=kOutput, calls=%fused_computation.135 | convolution fusion | flops 539492352 | bytes 3676164 | tf_op jit(solution)/shard_map/dot_general | solution.py:19
  103.5 3.2 %fusion.106 = f32[4,256,512]{2,1,0:T(8,128)} fusion(f32[512]{0:T(512)S(1)} %bitcast.196, f32[4,256]{1,0:T(4,128)S(1)} %add_rsqrt_fusion.7, bf16[4,3,512,512]{3,2,1,0:T(8,128)(2,1)} %all-gather.3.cloned.1.call-done, bf16[4,256,512]{2,1,0:T(8,128)(2,1)S(1)} %gather_fusion, pred[4]{0:T(512)(128)(4,1)S(1)} %get-tuple-element.204), kind=kOutput, calls=%fused_computation.136 | convolution fusion | flops 539492352 | bytes 3676164 | tf_op jit(solution)/shard_map/dot_general | solution.py:19
  106.7 4.5 %fusion.16 = (f32[4,256]{1,0:T(4,128)S(1)}, bf16[4,256,512]{2,1,0:T(8,128)(2,1)}) fusion(bf16[4,1,512,512]{3,2,1,0:T(8,128)(2,1)} %all-to-all-done, f32[4,256,512]{2,1,0:T(8,128)} %fusion.104, f32[4,256,512]{2,1,0:T(8,128)} %fusion.106, f32[512]{0:T(512)S(1)} %bitcast.197, f32[4,256]{1,0:T(4,128)S(1)} %add_rsqrt_fusion.7, ...), kind=kOutput, calls=%fused_computation.54 | convolution fusion | flops 1083702272 | bytes 8399872 | tf_op jit(solution)/shard_map/dot_general | solution.py:25
  111.2 3.1 %fusion.60 = f32[4,256,512]{2,1,0:T(8,128)} fusion(f32[4,256]{1,0:T(4,128)S(1)} %add_rsqrt_fusion.3, f32[512]{0:T(512)S(1)} %bitcast.198, bf16[4,3,512,512]{3,2,1,0:T(8,128)(2,1)} %all-gather.3.cloned.1.call-done, bf16[4,256,512]{2,1,0:T(8,128)(2,1)S(1)} %gather_fusion.1, pred[4]{0:T(512)(128)(4,1)S(1)} %get-tuple-element.203), kind=kOutput, calls=%fused_computation.107 | convolution fusion | flops 539492352 | bytes 3676164 | tf_op jit(solution)/shard_map/dot_general | solution.py:19
  114.3 3.2 %fusion.58 = f32[4,256,512]{2,1,0:T(8,128)} fusion(f32[4,256]{1,0:T(4,128)S(1)} %add_rsqrt_fusion.3, f32[512]{0:T(512)S(1)} %bitcast.199, bf16[4,3,512,512]{3,2,1,0:T(8,128)(2,1)} %all-gather.3.cloned.1.call-done, bf16[4,256,512]{2,1,0:T(8,128)(2,1)S(1)} %gather_fusion.1, pred[4]{0:T(512)(128)(4,1)S(1)} %get-tuple-element.203), kind=kOutput, calls=%fused_computation.106 | convolution fusion | flops 539492352 | bytes 3676164 | tf_op jit(solution)/shard_map/dot_general | solution.py:19
  117.5 4.6 %fusion.24 = (f32[4,256]{1,0:T(4,128)S(1)}, bf16[4,256,512]{2,1,0:T(8,128)(2,1)}) fusion(bf16[4,1,512,512]{3,2,1,0:T(8,128)(2,1)} %all-to-all-done, f32[4,256,512]{2,1,0:T(8,128)} %fusion.58, f32[4,256,512]{2,1,0:T(8,128)} %fusion.60, f32[4,256]{1,0:T(4,128)S(1)} %add_rsqrt_fusion.3, f32[512]{0:T(512)S(1)} %bitcast.200, ...), kind=kOutput, calls=%fused_computation.62 | convolution fusion | flops 1083702272 | bytes 8399872 | tf_op jit(solution)/shard_map/dot_general | solution.py:25
  122.1 3.5 %fusion.54 = f32[4,256,512]{2,1,0:T(8,128)} fusion(bf16[4,256,512]{2,1,0:T(8,128)(2,1)} %get-tuple-element.188, f32[4,256]{1,0:T(4,128)S(1)} %add_rsqrt_fusion.2, f32[512]{0:T(512)S(1)} %bitcast.189, bf16[4,3,512,512]{3,2,1,0:T(8,128)(2,1)} %all-gather.3.cloned.1.call-done), kind=kOutput, calls=%fused_computation.105 | convolution fusion | flops 538968064 | bytes 3676160 | tf_op jit(solution)/shard_map/dot_general | solution.py:19
  125.6 3.2 %fusion.52 = f32[4,256,512]{2,1,0:T(8,128)} fusion(bf16[4,256,512]{2,1,0:T(8,128)(2,1)S(1)} %copy-done.15, f32[4,256]{1,0:T(4,128)S(1)} %add_rsqrt_fusion.2, f32[512]{0:T(512)S(1)} %bitcast.190, bf16[4,3,512,512]{3,2,1,0:T(8,128)(2,1)} %all-gather.3.cloned.1.call-done), kind=kOutput, calls=%fused_computation.104 | convolution fusion | flops 538968064 | bytes 3676160 | tf_op jit(solution)/shard_map/dot_general | solution.py:19
  128.8 5.2 %fusion.27 = bf16[4,256,512]{2,1,0:T(8,128)(2,1)} fusion(bf16[4,256,512]{2,1,0:T(8,128)(2,1)} %get-tuple-element.188, f32[4,256,512]{2,1,0:T(8,128)} %fusion.52, f32[4,256,512]{2,1,0:T(8,128)} %fusion.54, f32[4,256]{1,0:T(4,128)S(1)} %add_rsqrt_fusion.2, f32[512]{0:T(512)S(1)} %bitcast.191, bf16[4,3,512,512]{3,2,1,0:T(8,128)(2,1)} %all-gather.3.cloned.1.call-done, ...), kind=kOutput, calls=%fused_computation.65 | convolution fusion | flops 1081081856 | bytes 8394752 | tf_op jit(solution)/shard_map/dot_general | solution.py:25
  134.1 2.3 fusion.131
  137.0 3.5 %fusion.82 = f32[4,256,512]{2,1,0:T(8,128)} fusion(bf16[4,256,512]{2,1,0:T(8,128)(2,1)} %get-tuple-element.190, f32[512]{0:T(512)S(1)} %bitcast.192, f32[4,256]{1,0:T(4,128)S(1)} %add_rsqrt_fusion.6, bf16[4,3,512,512]{3,2,1,0:T(8,128)(2,1)} %all-gather.3.cloned.1.call-done), kind=kOutput, calls=%fused_computation.119 | convolution fusion | flops 538968064 | bytes 3676160 | tf_op jit(solution)/shard_map/dot_general | solution.py:19
  140.5 3.4 %fusion.84 = f32[4,256,512]{2,1,0:T(8,128)} fusion(bf16[4,256,512]{2,1,0:T(8,128)(2,1)} %get-tuple-element.190, f32[512]{0:T(512)S(1)} %bitcast.193, f32[4,256]{1,0:T(4,128)S(1)} %add_rsqrt_fusion.6, bf16[4,3,512,512]{3,2,1,0:T(8,128)(2,1)} %all-gather.3.cloned.1.call-done), kind=kOutput, calls=%fused_computation.120 | convolution fusion | flops 538968064 | bytes 3676160 | tf_op jit(solution)/shard_map/dot_general | solution.py:19
  143.9 5.3 %fusion.19 = bf16[4,256,512]{2,1,0:T(8,128)(2,1)} fusion(bf16[4,256,512]{2,1,0:T(8,128)(2,1)} %get-tuple-element.190, f32[4,256,512]{2,1,0:T(8,128)} %fusion.82, f32[4,256,512]{2,1,0:T(8,128)} %fusion.84, f32[512]{0:T(512)S(1)} %bitcast.194, f32[4,256]{1,0:T(4,128)S(1)} %add_rsqrt_fusion.6, bf16[4,3,512,512]{3,2,1,0:T(8,128)(2,1)} %all-gather.3.cloned.1.call-done, ...), kind=kOutput, calls=%fused_computation.57 | convolution fusion | flops 1081081856 | bytes 8394752 | tf_op jit(solution)/shard_map/dot_general | solution.py:25
  149.3 2.4 fusion.125
  152.3 0.7 fusion.142
  153.1 0.6 broadcast_select_fusion.9
  154.0 39.3 %all-reduce.16 = (f32[8,18]{1,0:T(8,128)S(1)}, f32[8]{0:T(128)S(1)}) all-reduce(f32[8,18]{1,0:T(8,128)S(1)} %scatter-add.19, f32[8]{0:T(128)S(1)} %fusion.155), channel_id=1, replica_groups=mesh['section'=4,'dp'=8] {'section','dp'}, use_global_device_ids=true, to_apply=%region_18.20 | all-reduce | flops 152 | bytes 1216 | tf_op jit(solution)/shard_map/psum | solution.py:111
  193.3 0.7 broadcast_select_fusion.11
  194.1 0.6 broadcast_select_fusion.8
  195.4 0.6 broadcast_select_fusion.6
  196.0 0.6 broadcast_select_fusion.5
  196.7 0.6 broadcast_select_fusion.4
  197.4 0.6 broadcast_select_fusion.3
  198.1 0.6 broadcast_select_fusion.2
  200.8 0.6 copy-done.4
  201.4 3.1 %fusion.120 = f32[4,256,512]{2,1,0:T(8,128)} fusion(bf16[4,256,512]{2,1,0:T(8,128)(2,1)S(1)} %bitcast.175, bf16[4,3,512,512]{3,2,1,0:T(8,128)(2,1)} %all-gather.3.cloned.1.call-done), kind=kOutput, calls=%fused_computation.160 | convolution fusion | flops 536870912 | bytes 3670016 | tf_op jit(solution)/shard_map/dot_general | solution.py:19
  204.5 3.1 %fusion.118 = f32[4,256,512]{2,1,0:T(8,128)} fusion(bf16[4,256,512]{2,1,0:T(8,128)(2,1)S(1)} %bitcast.176, bf16[4,3,512,512]{3,2,1,0:T(8,128)(2,1)} %all-gather.3.cloned.1.call-done), kind=kOutput, calls=%fused_computation.158 | convolution fusion | flops 536870912 | bytes 3670016 | tf_op jit(solution)/shard_map/dot_general | solution.py:19
  207.6 5.2 %fusion.28 = (f32[4,256]{1,0:T(4,128)S(1)}, bf16[4,256,512]{2,1,0:T(8,128)(2,1)}) fusion(f32[4,256,512]{2,1,0:T(8,128)} %bitcast.179, bf16[4,1,512,512]{3,2,1,0:T(8,128)(2,1)} %all-to-all-done, f32[4,256,512]{2,1,0:T(8,128)} %fusion.120, f32[4,256,512]{2,1,0:T(8,128)} %fusion.118, bf16[4,256,512]{2,1,0:T(8,128)(2,1)S(1)} %bitcast.177, ...), kind=kOutput, calls=%fused_computation.66 | convolution fusion | flops 1080032256 | bytes 9441280 | tf_op jit(solution)/shard_map/dot_general | solution.py:25
  212.8 3.5 %fusion.48 = f32[4,256,512]{2,1,0:T(8,128)} fusion(bf16[4,256,512]{2,1,0:T(8,128)(2,1)} %get-tuple-element.196, f32[4,256]{1,0:T(4,128)S(1)} %add_rsqrt_fusion, f32[512]{0:T(512)S(1)} %bitcast.183, bf16[4,3,512,512]{3,2,1,0:T(8,128)(2,1)} %all-gather.3.cloned.1.call-done), kind=kOutput, calls=%fused_computation.103 | convolution fusion | flops 538968064 | bytes 3676160 | tf_op jit(solution)/shard_map/dot_general | solution.py:19
  216.3 3.2 %fusion.46 = f32[4,256,512]{2,1,0:T(8,128)} fusion(bf16[4,256,512]{2,1,0:T(8,128)(2,1)S(1)} %copy-done.14, f32[4,256]{1,0:T(4,128)S(1)} %add_rsqrt_fusion, f32[512]{0:T(512)S(1)} %bitcast.184, bf16[4,3,512,512]{3,2,1,0:T(8,128)(2,1)} %all-gather.3.cloned.1.call-done), kind=kOutput, calls=%fused_computation.102 | convolution fusion | flops 538968064 | bytes 3676160 | tf_op jit(solution)/shard_map/dot_general | solution.py:19
  219.5 3.8 %fusion.43 = f32[4,256]{1,0:T(4,128)S(1)} fusion(f32[4,256,512]{2,1,0:T(8,128)} %fusion.46, f32[4,256,512]{2,1,0:T(8,128)} %fusion.48, bf16[4,256,512]{2,1,0:T(8,128)(2,1)S(1)} %copy-done.14, f32[4,256]{1,0:T(4,128)S(1)} %add_rsqrt_fusion, f32[512]{0:T(512)S(1)} %bitcast.185, bf16[4,3,512,512]{3,2,1,0:T(8,128)(2,1)} %all-gather.3.cloned.1.call-done, ...), kind=kOutput, calls=%fused_computation.81 | convolution fusion | flops 1084226560 | bytes 8399360 | tf_op jit(solution)/shard_map/dot_general | solution.py:25
  223.2 3.0 %fusion.121 = f32[4,256,512]{2,1,0:T(8,128)} fusion(bf16[4,256,512]{2,1,0:T(8,128)(2,1)S(1)} %bitcast.172, bf16[4,3,512,512]{3,2,1,0:T(8,128)(2,1)} %all-gather.3.cloned.1.call-done), kind=kOutput, calls=%fused_computation.161 | convolution fusion | flops 536870912 | bytes 3670016 | tf_op jit(solution)/shard_map/dot_general | solution.py:19
  226.3 3.3 %fusion.119 = f32[4,256,512]{2,1,0:T(8,128)} fusion(bf16[4,256,512]{2,1,0:T(8,128)(2,1)S(1)} %bitcast.173, bf16[4,3,512,512]{3,2,1,0:T(8,128)(2,1)} %all-gather.3.cloned.1.call-done), kind=kOutput, calls=%fused_computation.159 | convolution fusion | flops 536870912 | bytes 3670016 | tf_op jit(solution)/shard_map/dot_general | solution.py:19
  229.5 4.4 %fusion.20 = (f32[4,256]{1,0:T(4,128)S(1)}, bf16[4,256,512]{2,1,0:T(8,128)(2,1)}) fusion(f32[4,256,512]{2,1,0:T(8,128)S(1)} %bitcast.178, bf16[4,1,512,512]{3,2,1,0:T(8,128)(2,1)} %all-to-all-done, f32[4,256,512]{2,1,0:T(8,128)} %fusion.121, f32[4,256,512]{2,1,0:T(8,128)} %fusion.119, bf16[4,256,512]{2,1,0:T(8,128)(2,1)S(1)} %bitcast.174, ...), kind=kOutput, calls=%fused_computation.58 | convolution fusion | flops 1080032256 | bytes 9441280 | tf_op jit(solution)/shard_map/dot_general | solution.py:25
  234.0 3.6 %fusion.68 = f32[4,256,512]{2,1,0:T(8,128)} fusion(bf16[4,256,512]{2,1,0:T(8,128)(2,1)} %get-tuple-element.198, f32[512]{0:T(512)S(1)} %bitcast.186, f32[4,256]{1,0:T(4,128)S(1)} %add_rsqrt_fusion.4, bf16[4,3,512,512]{3,2,1,0:T(8,128)(2,1)} %all-gather.3.cloned.1.call-done), kind=kOutput, calls=%fused_computation.111 | convolution fusion | flops 538968064 | bytes 3676160 | tf_op jit(solution)/shard_map/dot_general | solution.py:19
  237.6 3.2 %fusion.70 = f32[4,256,512]{2,1,0:T(8,128)} fusion(bf16[4,256,512]{2,1,0:T(8,128)(2,1)S(1)} %copy-done.13, f32[512]{0:T(512)S(1)} %bitcast.187, f32[4,256]{1,0:T(4,128)S(1)} %add_rsqrt_fusion.4, bf16[4,3,512,512]{3,2,1,0:T(8,128)(2,1)} %all-gather.3.cloned.1.call-done), kind=kOutput, calls=%fused_computation.112 | convolution fusion | flops 538968064 | bytes 3676160 | tf_op jit(solution)/shard_map/dot_general | solution.py:19
  240.8 3.8 %fusion.37 = f32[4,256]{1,0:T(4,128)S(1)} fusion(f32[4,256,512]{2,1,0:T(8,128)} %fusion.68, f32[4,256,512]{2,1,0:T(8,128)} %fusion.70, bf16[4,256,512]{2,1,0:T(8,128)(2,1)S(1)} %copy-done.13, f32[512]{0:T(512)S(1)} %bitcast.188, f32[4,256]{1,0:T(4,128)S(1)} %add_rsqrt_fusion.4, bf16[4,3,512,512]{3,2,1,0:T(8,128)(2,1)} %all-gather.3.cloned.1.call-done, ...), kind=kOutput, calls=%fused_computation.75 | convolution fusion | flops 1084226560 | bytes 8399360 | tf_op jit(solution)/shard_map/dot_general | solution.py:25
  245.0 0.6 pad_maximum_fusion
  (73 shorter events, 5.0 us)
Async XLA Ops:
  7.2 191.7 %copy-start = (bf16[18,512]{1,0:T(8,128)(2,1)S(1)}, bf16[18,512]{1,0:T(8,128)(2,1)}, u32[]{:S(2)}) copy-start(bf16[18,512]{1,0:T(8,128)(2,1)} %param.43) | copy-start | bytes 55300
  7.2 93.2 %all-gather.3.cloned.1.call-start = ((), (), s32[]{:S(2)}) async-start(), calls=%async_computation.1 | async-start | bytes 7864320 | tf_op jit(solution)/shard_map/all_gather | solution.py:89
  10.5 5.3 %copy-start.7 = (s32[8]{0:T(128)S(1)}, s32[8]{0:T(128)}, u32[]{:S(2)}) copy-start(s32[8]{0:T(128)} %param.37) | copy-start | bytes 100
  10.5 15.9 %copy-start.8 = (s32[8,4]{0,1:T(4,128)S(1)}, s32[8,4]{0,1:T(4,128)}, u32[]{:S(2)}) copy-start(s32[8,4]{0,1:T(4,128)} %param.36) | copy-start | bytes 388
  10.5 96.1 %all-to-all-start = ((bf16[4,1,512,512]{3,2,1,0:T(8,128)(2,1)}), bf16[4,1,512,512]{3,2,1,0:T(8,128)(2,1)}, u32[]{:S(2)}, u32[]{:S(2)}) async-start(bf16[4,1,512,512]{3,2,1,0:T(8,128)(2,1)} %stack.4), calls=%async_computation | async-start | bytes 4194304 | tf_op jit(solution)/shard_map/all_to_all | solution.py:91
  26.7 13.4 %copy-start.10 = (bf16[1,512]{1,0:T(2,128)(2,1)S(1)}, bf16[1,512]{1,0:T(2,128)(2,1)}, u32[]{:S(2)}) copy-start(bf16[1,512]{1,0:T(2,128)(2,1)} %param.40) | copy-start | bytes 3076
  26.7 34.9 %copy-start.9 = (s32[2]{0:T(128)S(1)}, s32[2]{0:T(128)}, u32[]{:S(2)}) copy-start(s32[2]{0:T(128)} %constant.321.clone.1) | copy-start | bytes 28
  30.7 76.0 %copy-start.5 = (bf16[4,256,512]{2,1,0:T(8,128)(2,1)}, bf16[4,256,512]{2,1,0:T(8,128)(2,1)S(1)}, u32[]{:S(2)}) copy-start(bf16[4,256,512]{2,1,0:T(8,128)(2,1)S(1)} %gather_fusion) | copy-start | bytes 3145732
  122.1 3.5 %copy-start.15 = (bf16[4,256,512]{2,1,0:T(8,128)(2,1)S(1)}, bf16[4,256,512]{2,1,0:T(8,128)(2,1)}, u32[]{:S(2)}) copy-start(bf16[4,256,512]{2,1,0:T(8,128)(2,1)} %get-tuple-element.188) | copy-start | bytes 3145732
  128.8 5.2 %copy-start.11 = (bf16[512,18]{0,1:T(8,128)(2,1)S(1)}, bf16[512,18]{0,1:T(8,128)(2,1)}, u32[]{:S(2)}) copy-start(bf16[512,18]{0,1:T(8,128)(2,1)} %param.41) | copy-start | bytes 55300
  128.8 5.2 %copy-start.12 = (f32[18]{0:T(128)S(1)}, f32[18]{0:T(128)}, u32[]{:S(2)}) copy-start(f32[18]{0:T(128)} %param.42) | copy-start | bytes 220
  199.4 1.4 copy-start.2
  200.0 1.4 copy-start.4
  212.8 3.5 %copy-start.14 = (bf16[4,256,512]{2,1,0:T(8,128)(2,1)S(1)}, bf16[4,256,512]{2,1,0:T(8,128)(2,1)}, u32[]{:S(2)}) copy-start(bf16[4,256,512]{2,1,0:T(8,128)(2,1)} %get-tuple-element.196) | copy-start | bytes 3145732
  226.3 3.3 %copy-start.3 = (f32[1024,512]{1,0:T(8,128)S(1)}, f32[1024,512]{1,0:T(8,128)}, u32[]{:S(2)}) copy-start(f32[1024,512]{1,0:T(8,128)} %copy-done.2) | copy-start | bytes 6291460
  233.9 3.6 %copy-start.13 = (bf16[4,256,512]{2,1,0:T(8,128)(2,1)S(1)}, bf16[4,256,512]{2,1,0:T(8,128)(2,1)}, u32[]{:S(2)}) copy-start(bf16[4,256,512]{2,1,0:T(8,128)(2,1)} %get-tuple-element.198) | copy-start | bytes 3145732
  237.6 3.2 %copy-start.6 = (bf16[4,256,512]{2,1,0:T(8,128)(2,1)S(1)}, bf16[4,256,512]{2,1,0:T(8,128)(2,1)}, u32[]{:S(2)}) copy-start(bf16[4,256,512]{2,1,0:T(8,128)(2,1)} %copy-done.5) | copy-start | bytes 3145732
  240.8 4.9 %copy-start.1 = (bf16[18,512]{1,0:T(8,128)(2,1)S(1)}, bf16[18,512]{1,0:T(8,128)(2,1)}, u32[]{:S(2)}) copy-start(bf16[18,512]{1,0:T(8,128)(2,1)} %param.43) | copy-start | bytes 55300
Sparse Core Ops, SparseCore 0:
  9.8 90.4 all-gather.2
